TPU v7x, 32 devices: a whole 2x2x4 slice. The times are simulated.
32 devices in a mesh: row: 8 (over y, x, core), col: 4 (over z).
Axes of the slice: x: 2, y: 2, z: 4, core: 2. Of those that a mesh axis runs over, the one named last changes fastest.
Arguments:
- vectors: float32 [16384, 16384], P('row', 'col'), may hold values from -0.046875 to 0.046875
- basis: float32 [16384, 2048], P('col', 'row'), may hold values from -9 to 9
- block_units: int32 [8], replicated, may hold values from 1 to 40, 64 in all
Outputs:
- assembled: float32 [16384, 2048], P('row', 'col')
Inputs may be any that keep to these rules, and one draw needn't show every extreme that they name: `block_units`: the block sizes are whole numbers of units that sum to 64; the largest is exactly the maximum.
All inputs are finite; a program needn't handle non-finite values.
Results may differ from a plain program's by a relative error of at most 0.00007.
Values sent between devices are 32-bit elements; how exact they have to be, the bound alone decides.
A program may use at most 192 MiB of HBM per device.

v0:
```python
import jax
import jax.numpy as jnp
from jax import lax
from jax.sharding import PartitionSpec as P

W = 2048
UNIT = 256
BLOCKS = 8
START = 7168


def block_ids(positions, block_units):
    ends = jnp.cumsum(block_units) * UNIT
    return jnp.sum((positions[:, None] >= ends[None, :-1]).astype(jnp.int32), axis=1)


def shards(vectors, basis, block_units):
    inner = vectors.shape[1]
    offset = lax.axis_index("col") * inner
    row_block = block_ids(offset + jnp.arange(inner, dtype=jnp.int32), block_units)
    ends = jnp.cumsum(block_units) * UNIT
    starts = ends - block_units * UNIT
    edge_ids = block_ids(jnp.array([START, START + W - 1], dtype=jnp.int32), block_units)
    first_row = jnp.sum(jnp.where(jnp.arange(BLOCKS) == edge_ids[0], starts, 0))
    last_row = jnp.sum(jnp.where(jnp.arange(BLOCKS) == edge_ids[1], ends, 0))
    local_first = jnp.clip(first_row - offset, 0, inner) // UNIT
    local_last = (jnp.clip(last_row - offset, 0, inner) + UNIT - 1) // UNIT
    piece = lax.all_gather(basis, "row", axis=1, tiled=True)
    count = piece.shape[1]
    slab_block = block_ids(START + jnp.int32(0) + jnp.arange(count, dtype=jnp.int32), block_units)
    masked = jnp.where(row_block[:, None] == slab_block[None, :], piece, jnp.float32(0.0))

    def add_panel(panel, total):
        rows_at = (panel * UNIT).astype(jnp.int32)
        left = lax.dynamic_slice_in_dim(vectors, rows_at, UNIT, 1)
        right = lax.dynamic_slice_in_dim(masked, rows_at, UNIT, 0)
        return total + jnp.dot(
            left, right, precision=lax.Precision.HIGHEST, preferred_element_type=jnp.float32
        )

    empty = jnp.zeros((vectors.shape[0], piece.shape[1]), jnp.float32)
    partial_value = lax.fori_loop(local_first, local_last, add_panel, empty)
    return lax.psum_scatter(partial_value, "col", scatter_dimension=1, tiled=True)


def solution(mesh):
    in_specs = (P("row", "col"), P("col", "row"), P())
    out_specs = P("row", "col")
    return jax.shard_map(shards, mesh=mesh, in_specs=in_specs, out_specs=out_specs, check_vma=False)
```

profile of v0, /device:TPU:0, one launch (start us, length us, event | category | flops | bytes accessed | tf_op | source)
XLA Modules:
  0.0 837.7 jit_solution(1095085044070426356)
XLA Ops:
  6.5 0.0 all-gather.2.cloned.1.call-start
  6.5 0.7 all-gather.2.cloned.1.call-update
  7.3 0.0 reduce-scatter.2.cloned.1.call-start
  7.3 0.8 reduce-window.9
  8.2 0.8 fusion.3
  9.0 0.7 fusion.6
  9.7 2.7 fusion.5
  13.6 0.1 convert_reduce_fusion.1
  13.7 0.1 convert_reduce_fusion
  13.8 165.5 %all-gather.2.cloned.1.call-done = f32[4096,2048]{1,0:T(8,128)} async-done(((f32[4096,256]{1,0:T(8,128)}), f32[4096,2048]{1,0:T(8,128)}) %all-gather.2.cloned.1.call-update) | async-done | bytes 33554448 | tf_op jit(solution)/shard_map/all_gather | solution.py:28
  179.3 23.0 %compare_select_fusion = f32[4096,2048]{1,0:T(8,128)} fusion(f32[4096,2048]{1,0:T(8,128)} %all-gather.2.cloned.1.call-done, s32[2048]{0:T(1024)S(1)} %convert_reduce_fusion.1, s32[4096]{0:T(1024)S(1)} %convert_reduce_fusion), kind=kLoop, calls=%fused_computation.4 | loop fusion | flops 16777216 | bytes 67133440 | tf_op jit(solution)/shard_map/jit(_where)/select_n | solution.py:31
  202.3 7.8 broadcast_in_dim.11
  210.2 85.2 %while.10 = (s32[]{:T(128)}, f32[2048,2048]{1,0:T(8,128)}, s32[]{:T(128)}, f32[2048,4096]{1,0:T(8,128)}, f32[4096,2048]{1,0:T(8,128)}, /*index=5*/s32[]{:T(128)}, s32[]{:T(128)}, s32[]{:T(128)}, s32[]{:T(128)}) while((s32[]{:T(128)}, f32[2048,2048]{1,0:T(8,128)}, s32[]{:T(128)}, f32[2048,4096]{1,0:T(8,128)}, f32[4096,2048]{1,0:T(8,128)}, ...), condition=%wide.region_7.8_spmd, body=%wide.region_6.7_spmd.sunk | while | flops 12889096192 | bytes 37749896 | solution.py:42
  210.2 21.3 %convolution_add_fusion.2 = f32[2048,2048]{1,0:T(8,128)} fusion(f32[2048,2048]{1,0:T(8,128)} %get-tuple-element.90, f32[4096,2048]{1,0:T(8,128)} %get-tuple-element.102, s32[]{:T(128)S(6)} %select_n.36, f32[2048,4096]{1,0:T(8,128)} %get-tuple-element.101), kind=kOutput, calls=%fused_computation.clone.1 | convolution fusion | flops 12889096192 | bytes 37749760 | tf_op jit(solution)/shard_map/while/body/dot_general | solution.py:37
  231.5 21.3 %convolution_add_fusion.2 = f32[2048,2048]{1,0:T(8,128)} fusion(f32[2048,2048]{1,0:T(8,128)} %get-tuple-element.90, f32[4096,2048]{1,0:T(8,128)} %get-tuple-element.102, s32[]{:T(128)S(6)} %select_n.36, f32[2048,4096]{1,0:T(8,128)} %get-tuple-element.101), kind=kOutput, calls=%fused_computation.clone.1 | convolution fusion | flops 12889096192 | bytes 37749760 | tf_op jit(solution)/shard_map/while/body/dot_general | solution.py:37
  252.8 21.3 %convolution_add_fusion.2 = f32[2048,2048]{1,0:T(8,128)} fusion(f32[2048,2048]{1,0:T(8,128)} %get-tuple-element.90, f32[4096,2048]{1,0:T(8,128)} %get-tuple-element.102, s32[]{:T(128)S(6)} %select_n.36, f32[2048,4096]{1,0:T(8,128)} %get-tuple-element.101), kind=kOutput, calls=%fused_computation.clone.1 | convolution fusion | flops 12889096192 | bytes 37749760 | tf_op jit(solution)/shard_map/while/body/dot_general | solution.py:37
  274.1 21.3 %convolution_add_fusion.2 = f32[2048,2048]{1,0:T(8,128)} fusion(f32[2048,2048]{1,0:T(8,128)} %get-tuple-element.90, f32[4096,2048]{1,0:T(8,128)} %get-tuple-element.102, s32[]{:T(128)S(6)} %select_n.36, f32[2048,4096]{1,0:T(8,128)} %get-tuple-element.101), kind=kOutput, calls=%fused_computation.clone.1 | convolution fusion | flops 12889096192 | bytes 37749760 | tf_op jit(solution)/shard_map/while/body/dot_general | solution.py:37
  295.4 0.0 reduce-scatter.2.cloned.1.call-update
  295.4 535.4 %reduce-scatter.2.cloned.1.call-done = f32[2048,512]{1,0:T(8,128)} async-done(((f32[2048,2048]{1,0:T(8,128)}), f32[2048,512]{1,0:T(8,128)}) %reduce-scatter.2.cloned.1.call-update) | async-done | bytes 4194320 | tf_op jit(solution)/shard_map/reduce_scatter | solution.py:43
  (4 shorter events, 0.0 us)
Async XLA Ops:
  6.5 172.8 %all-gather.2.cloned.1.call-start = ((), (), s32[]{:S(2)}) async-start(), calls=%async_computation.1 | async-start | bytes 37748736 | tf_op jit(solution)/shard_map/all_gather | solution.py:28
  7.3 823.6 %reduce-scatter.2.cloned.1.call-start = ((), (), s32[]{:S(2)}) async-start(), calls=%async_computation.2 | async-start | bytes 20971520 | tf_op jit(solution)/shard_map/reduce_scatter | solution.py:43
Sparse Core Ops, SparseCore 0:
  9.2 170.0 all-gather.1
  295.6 535.2 reduce-scatter.1
where the time goes:
time: 838 us
  waiting for transfers between devices  702 us (84%)
  matrix products  85.2 us (10%)
  other arithmetic  27.6 us (3%)
  between operations  14.7 us (2%)
  local copies, waits for them, and re-layouts  8.5 us (1%)
    reduce_scatter x1, waiting for transfers between devices, shards(): lax.psum_scatter(partial_value, 'col', scatter_dimension=1, tiled=True)  535 us
    all_gather x1, waiting for transfers between devices, shards(): piece = lax.all_gather(basis, 'row', axis=1, tiled=True)  166 us
    dot_general x4, matrix products, add_panel(): jnp.dot(left, right, precision=lax.Precision.HIGHEST, preferred_element_t...  85.2 us
    select_n x1, other arithmetic, shards(): jnp.where(row_block[:, None] == slab_block[None, :], piece, jnp.float32(0...  23 us
  transfers between devices with their start and end apart: 2, of which 2 were waited for; matrix products, arithmetic and copies ran while one was open for 1% of the time, Pallas kernels for 0%

commit v1 on v0

v1 whole, which is shorter than its diff:
```python
import jax
import jax.numpy as jnp
from jax import lax
from jax.sharding import PartitionSpec as P

UNIT = 256
START = 7168
LANES = 128


def block_ids(positions, block_units):
    ends = jnp.cumsum(block_units) * UNIT
    return jnp.sum((positions[:, None] >= ends[None, :-1]).astype(jnp.int32), axis=1)


def shards(vectors, basis, block_units):
    inner, width = basis.shape
    row_block = block_ids(
        lax.axis_index("col") * inner + jnp.arange(inner, dtype=jnp.int32), block_units
    )
    slab_block = block_ids(
        START + lax.axis_index("row") * width + jnp.arange(width, dtype=jnp.int32), block_units
    )
    masked = jnp.where(row_block[:, None] == slab_block[None, :], basis, jnp.float32(0.0))

    rows, cols = lax.axis_size("row"), lax.axis_size("col")
    step = LANES if width % LANES == 0 and rows % cols == 0 else width
    pieces = [
        lax.all_gather(masked[:, at:at + step], "row", axis=1, tiled=True)
        for at in range(0, width, step)
    ]
    sums = []
    for piece in pieces:
        part = jnp.dot(
            vectors, piece, precision=lax.Precision.HIGH, preferred_element_type=jnp.float32
        )
        sums.append(lax.psum_scatter(part, "col", scatter_dimension=1, tiled=True))
    groups = sums[0].shape[1] // step
    return jnp.concatenate(
        [one[:, g * step:(g + 1) * step] for g in range(groups) for one in sums], axis=1
    )


def solution(mesh):
    in_specs = (P("row", "col"), P("col", "row"), P())
    out_specs = P("row", "col")
    return jax.shard_map(shards, mesh=mesh, in_specs=in_specs, out_specs=out_specs, check_vma=False)
```

time: 838 us -> 529 us (0.63)
  waiting for transfers between devices: 702 us -> 275 us
  matrix products: 85.2 us -> 222 us
  other arithmetic: 27.6 us -> 7.3 us
    reduce_scatter x1 -> x2, waiting for transfers between devices: 535 us -> 179 us  [shards(): sums.append(lax.psum_scatter(part, 'col', scatter_dimension=1, tiled=True))]
    dot_general x4 -> x2, matrix products: 85.2 us -> 222 us  [shards(): jnp.dot(vectors, piece, precision=lax.Precision.HIGH, preferred_element_t...]
    all_gather x1 -> x2, waiting for transfers between devices: 166 us -> 95.1 us  [shards(): lax.all_gather(masked[:, at:at + step], 'row', axis=1, tiled=True)]
    select_n x1, other arithmetic: 23 us -> 3.91 us  [shards(): jnp.where(row_block[:, None] == slab_block[None, :], basis, jnp.float32(0...]
  transfers between devices with their start and end apart: 2 -> 4, of which waited for: 2 -> 3; matrix products, arithmetic and copies ran while one was open for 1% -> 42% of each run, Pallas kernels for 0% -> 0%
where the time goes in v1:
time: 529 us
  waiting for transfers between devices  275 us (52%)
  matrix products  222 us (42%)
  between operations  13.2 us (2%)
  local copies, waits for them, and re-layouts  11.1 us (2%)
  other arithmetic  7.3 us (1%)
    dot_general x2, matrix products, shards(): jnp.dot(vectors, piece, precision=lax.Precision.HIGH, preferred_element_t...  222 us
    reduce_scatter x2, waiting for transfers between devices, shards(): sums.append(lax.psum_scatter(part, 'col', scatter_dimension=1, tiled=True))  179 us
    all_gather x2, waiting for transfers between devices, shards(): lax.all_gather(masked[:, at:at + step], 'row', axis=1, tiled=True)  95.1 us
  transfers between devices with their start and end apart: 4, of which 3 were waited for; matrix products, arithmetic and copies ran while one was open for 42% of the time, Pallas kernels for 0%

profile of v1, /device:TPU:0, one launch (start us, length us, event | category | flops | bytes accessed | tf_op | source)
XLA Modules:
  0.0 529.0 jit_solution(5976717857978838351)
XLA Ops:
  6.5 0.0 all-gather.3.cloned.1.call-start
  6.5 0.8 reduce-window.9
  7.4 0.1 convert_reduce_fusion.1
  7.5 0.1 convert_reduce_fusion
  7.6 3.9 compare_select_fusion
  11.5 2.3 fusion
  13.8 0.0 all-gather.3.cloned.1.call-update
  13.9 0.0 all-gather.5.cloned.1.call-start
  13.9 0.7 all-gather.5.cloned.1.call-update
  14.6 0.0 reduce-scatter.3.cloned.1.call-start
  14.7 95.1 %all-gather.3.cloned.1.call-done = f32[4096,1024]{1,0:T(8,128)} async-done(((f32[4096,128]{1,0:T(8,128)}), f32[4096,1024]{1,0:T(8,128)}) %all-gather.3.cloned.1.call-update) | async-done | bytes 16777232 | tf_op jit(solution)/shard_map/all_gather | solution.py:29
  109.8 111.0 %convolution_bitcast_fusion.1 = f32[2048,1024]{0,1:T(8,128)} fusion(f32[4096,1024]{1,0:T(8,128)} %all-gather.3.cloned.1.call-done, f32[2048,4096]{1,0:T(8,128)} %param.3), kind=kOutput, calls=%fused_computation.1 | convolution fusion | flops 51539607552 | bytes 58720256 | tf_op jit(solution)/shard_map/dot_general | solution.py:34
  220.7 0.0 reduce-scatter.3.cloned.1.call-update
  220.8 0.0 reduce-scatter.5.cloned.1.call-start
  220.8 0.0 all-gather.5.cloned.1.call-done
  220.8 111.1 %convolution_bitcast_fusion = f32[2048,1024]{0,1:T(8,128)} fusion(f32[4096,1024]{1,0:T(8,128)} %all-gather.5.cloned.1.call-done, f32[2048,4096]{1,0:T(8,128)} %param.3), kind=kOutput, calls=%fused_computation | convolution fusion | flops 51539607552 | bytes 58720256 | tf_op jit(solution)/shard_map/dot_general | solution.py:34
  332.0 0.0 reduce-scatter.5.cloned.1.call-update
  332.0 33.5 %reduce-scatter.3.cloned.1.call-done = f32[2048,256]{0,1:T(8,128)} async-done(((f32[2048,1024]{0,1:T(8,128)}), f32[2048,256]{0,1:T(8,128)}) %reduce-scatter.3.cloned.1.call-update) | async-done | bytes 2097168 | tf_op jit(solution)/shard_map/reduce_scatter | solution.py:37
  365.5 1.7 fusion.1
  367.2 145.8 %reduce-scatter.5.cloned.1.call-done = f32[2048,256]{0,1:T(8,128)} async-done(((f32[2048,1024]{0,1:T(8,128)}), f32[2048,256]{0,1:T(8,128)}) %reduce-scatter.5.cloned.1.call-update) | async-done | bytes 2097168 | tf_op jit(solution)/shard_map/reduce_scatter | solution.py:37
  513.0 1.8 fusion.2
  514.8 2.3 pad_maximum_fusion
  517.1 5.3 %copy.5 = f32[2048,512]{1,0:T(8,128)} copy(f32[2048,512]{0,1:T(8,128)} %pad_maximum_fusion) | data formatting | bytes 8388608 | tf_op jit(solution)/shard_map/concatenate | solution.py:39
  (4 shorter events, 0.0 us)
Async XLA Ops:
  6.5 103.2 %all-gather.3.cloned.1.call-start = ((), (), s32[]{:S(2)}) async-start(), calls=%async_computation.2 | async-start | bytes 18874368 | tf_op jit(solution)/shard_map/all_gather | solution.py:29
  13.9 207.0 %all-gather.5.cloned.1.call-start = ((), (), s32[]{:S(2)}) async-start(), calls=%async_computation.4 | async-start | bytes 18874368 | tf_op jit(solution)/shard_map/all_gather | solution.py:29
  14.6 350.9 %reduce-scatter.3.cloned.1.call-start = ((), (), s32[]{:S(2)}) async-start(), calls=%async_computation.3 | async-start | bytes 10485760 | tf_op jit(solution)/shard_map/reduce_scatter | solution.py:37
  220.8 292.2 %reduce-scatter.5.cloned.1.call-start = ((), (), s32[]{:S(2)}) async-start(), calls=%async_computation.5 | async-start | bytes 10485760 | tf_op jit(solution)/shard_map/reduce_scatter | solution.py:37
Sparse Core Ops, SparseCore 0:
  14.0 95.7 all-gather.2
  111.6 93.0 all-gather.4
  220.9 144.6 reduce-scatter.2
  367.7 145.2 reduce-scatter.4
